TPU v7x, 32 devices: a 4x4x1 block of a 4x4x8 slice. The times are simulated.
32 devices in a mesh: ens: 1 (over z), feat: 32 (over y, x, core).
Axes of the slice: x: 4, y: 4, z: 1, core: 2. Of those that a mesh axis runs over, the one named last changes fastest.
The devices are a block of a 4x4x8 slice.
Arguments:
- particles: float32 [256, 49152], P('ens', 'feat')
- prec_diag: float32 [49152], P(('ens', 'feat'))
- low_factor: bfloat16 [49152, 128], P(('ens', 'feat'))
- prior_mean: float32 [49152], P(('ens', 'feat'))
- data_mat: bfloat16 [768, 49152], P('ens', 'feat')
- labels: int32 [768], P('ens')
Outputs:
- output: float32 [256, 49152], P('ens', 'feat')
All inputs are finite; a program needn't handle non-finite values.
Results may differ from a plain program's by a relative error of at most 0.001.
Values are sent between devices in bfloat16 or wider.
A program may use at most 768 MiB of HBM per device.

v0:
```python
import math
import jax
import jax.numpy as jnp
from jax import lax
from jax.sharding import PartitionSpec as P

NUM_STEPS = 3
DIMS_NT = (((1,), (1,)), ((), ()))


def solution(mesh):
    feat_size = mesh.shape["feat"]

    def local_run(particles, prec_diag, low_factor, prior_mean, data_mat, labels):
        n_part, dim_local = particles.shape
        dim_full = dim_local * feat_size
        m_rows = data_mat.shape[0]
        band_width = 2.0 * dim_full
        step_size = dim_full / 4.0
        lik_weight = 2.0 / math.sqrt(m_rows * dim_full)
        targets = labels.astype(jnp.float32)[None, :]
        state = particles
        for step_idx in range(NUM_STEPS):
            part_bf = state.astype(jnp.bfloat16)
            centred = state - prior_mean
            projected = lax.psum(jnp.dot(centred.astype(jnp.bfloat16), low_factor, preferred_element_type=jnp.float32), "feat")
            gram_mat = lax.psum(lax.dot_general(part_bf, part_bf, DIMS_NT, preferred_element_type=jnp.float32), "feat")
            logits = lax.psum(lax.dot_general(part_bf, data_mat, DIMS_NT, preferred_element_type=jnp.float32), "feat")
            sq_norm = jnp.diagonal(gram_mat)
            sq_dist = jnp.maximum(sq_norm[:, None] + sq_norm[None, :] - 2.0 * gram_mat, 0.0)
            kernel = jnp.exp(-sq_dist / band_width)
            residual = targets - jax.nn.sigmoid(logits)
            low_rank = lax.dot_general(projected.astype(jnp.bfloat16), low_factor, DIMS_NT, preferred_element_type=jnp.float32)
            lik_term = jnp.dot(residual.astype(jnp.bfloat16), data_mat, preferred_element_type=jnp.float32)
            log_grad = lik_weight * lik_term - centred * prec_diag - low_rank
            kern_bf = kernel.astype(jnp.bfloat16)
            driving = jnp.dot(kern_bf, log_grad.astype(jnp.bfloat16), preferred_element_type=jnp.float32)
            pulled = jnp.dot(kern_bf, part_bf, preferred_element_type=jnp.float32)
            row_sum = jnp.sum(kernel, axis=1, keepdims=True)
            update_dir = (driving + (2.0 / band_width) * (row_sum * state - pulled)) / n_part
            state = state + step_size * update_dir
        return state

    return jax.shard_map(
        local_run,
        mesh=mesh,
        in_specs=(P("ens", "feat"), P(("ens", "feat")), P(("ens", "feat"), None),
                  P(("ens", "feat")), P("ens", "feat"), P("ens")),
        out_specs=P("ens", "feat"),
        check_vma=False,
    )
```

profile of v0, /device:TPU:97, one launch (start us, length us, event | category | flops | bytes accessed | tf_op | source)
XLA Modules:
  0.0 352.3 jit_solution(12270509106967922629)
XLA Ops:
  6.5 0.0 copy-start
  6.6 0.0 all-reduce.14.cloned.1.call-start
  6.6 3.2 fusion.61
  9.7 0.0 copy-done
  9.7 0.0 copy-done.3
  9.7 0.0 copy-start.4
  9.7 0.0 copy-start.8
  9.7 1.7 fusion.59
  11.4 0.1 all-reduce.14.cloned.1.call-update
  11.5 0.1 all-reduce.12.cloned.1.call-start
  11.6 0.0 copy-done.9
  11.6 0.0 copy-start.10
  11.6 1.8 fusion.21
  13.4 51.3 %all-reduce.15 = bf16[256,128]{1,0:T(8,128)(2,1)S(1)} all-reduce(f32[256,128]{1,0:T(8,128)S(1)} %fusion.21), channel_id=1, replica_groups=mesh['ens'=1,'feat'=32] {'feat'}, use_global_device_ids=true, to_apply=%region_2.0 | all-reduce | flops 32768 | bytes 196608 | tf_op jit(solution)/shard_map/psum | solution.py:26
  64.8 46.1 %all-reduce.14.cloned.1.call-done = (f32[256,768]{1,0:T(8,128)}, f32[256,256]{1,0:T(8,128)}) async-done(((f32[256,768]{1,0:T(8,128)}, f32[256,256]{1,0:T(8,128)}), (f32[256,768]{1,0:T(8,128)}, f32[256,256]{1,0:T(8,128)})) %all-reduce.14.cloned.1.call-update) | async-done | bytes 1048592 | tf_op jit(solution)/shard_map/psum | solution.py:28
  110.8 2.6 gather_fusion
  113.4 1.2 fusion.33
  114.6 0.0 copy-done.10
  114.6 0.0 copy-start.5
  114.6 3.7 %fusion.14 = f32[256,1536]{1,0:T(8,128)} fusion(bf16[768,1536]{1,0:T(8,128)(2,1)S(1)} %copy-done, f32[256,1536]{1,0:T(8,128)} %param.6, f32[1536]{0:T(1024)S(1)} %copy-done.10, f32[1536]{0:T(1024)S(1)} %copy-done.8, f32[256,768]{1,0:T(8,128)} %get-tuple-element.9, f32[768]{0:T(1024)S(1)} %convert_element_type.59), kind=kOutput, calls=%fused_computation.26 | convolution fusion | flops 606535680 | bytes 6306816 | tf_op jit(solution)/shard_map/dot_general | solution.py:34
  118.2 0.0 copy-done.5
  118.2 3.1 fusion.20
  121.4 3.0 fusion.13
  124.4 0.0 copy-start.2
  124.4 1.7 fusion.51
  126.1 1.1 fusion.53
  127.2 0.1 all-reduce.12.cloned.1.call-update
  127.3 0.1 all-reduce.10.cloned.1.call-start
  127.3 1.8 fusion.22
  129.1 47.0 %all-reduce.16 = bf16[256,128]{1,0:T(8,128)(2,1)S(1)} all-reduce(f32[256,128]{1,0:T(8,128)S(1)} %fusion.22), channel_id=1, replica_groups=mesh['ens'=1,'feat'=32] {'feat'}, use_global_device_ids=true, to_apply=%region_6.7 | all-reduce | flops 32768 | bytes 196608 | tf_op jit(solution)/shard_map/psum | solution.py:26
  176.1 46.0 %all-reduce.12.cloned.1.call-done = (f32[256,768]{1,0:T(8,128)}, f32[256,256]{1,0:T(8,128)}) async-done(((f32[256,768]{1,0:T(8,128)}, f32[256,256]{1,0:T(8,128)}), (f32[256,768]{1,0:T(8,128)}, f32[256,256]{1,0:T(8,128)})) %all-reduce.12.cloned.1.call-update) | async-done | bytes 1048592 | tf_op jit(solution)/shard_map/psum | solution.py:28
  222.1 3.7 %fusion.9 = f32[256,1536]{1,0:T(8,128)} fusion(bf16[768,1536]{1,0:T(8,128)(2,1)S(1)} %copy-done, f32[256,1536]{1,0:T(8,128)} %copy-done.2, f32[1536]{0:T(1024)S(1)} %copy-done.10, f32[1536]{0:T(1024)S(1)} %copy-done.8, f32[256,768]{1,0:T(8,128)} %get-tuple-element.7, f32[768]{0:T(1024)S(1)} %convert_element_type.59), kind=kOutput, calls=%fused_computation.18 | convolution fusion | flops 606535680 | bytes 6306816 | tf_op jit(solution)/shard_map/dot_general | solution.py:34
  225.8 0.0 copy-done.6
  225.8 2.3 gather_fusion.1
  228.1 0.2 fusion.35
  228.4 3.1 fusion.19
  231.5 3.0 fusion.8
  234.5 1.7 fusion.46
  236.2 1.1 fusion.48
  237.3 0.1 all-reduce.10.cloned.1.call-update
  237.4 1.8 fusion.23
  239.2 46.6 %all-reduce.17 = bf16[256,128]{1,0:T(8,128)(2,1)S(1)} all-reduce(f32[256,128]{1,0:T(8,128)S(1)} %fusion.23), channel_id=1, replica_groups=mesh['ens'=1,'feat'=32] {'feat'}, use_global_device_ids=true, to_apply=%region_10.11 | all-reduce | flops 32768 | bytes 196608 | tf_op jit(solution)/shard_map/psum | solution.py:26
  285.7 46.5 %all-reduce.10.cloned.1.call-done = (f32[256,768]{1,0:T(8,128)}, f32[256,256]{1,0:T(8,128)}) async-done(((f32[256,768]{1,0:T(8,128)}, f32[256,256]{1,0:T(8,128)}), (f32[256,768]{1,0:T(8,128)}, f32[256,256]{1,0:T(8,128)})) %all-reduce.10.cloned.1.call-update) | async-done | bytes 1048592 | tf_op jit(solution)/shard_map/psum | solution.py:28
  332.3 3.7 %fusion.4 = f32[256,1536]{1,0:T(8,128)} fusion(bf16[768,1536]{1,0:T(8,128)(2,1)S(1)} %copy-done, f32[256,1536]{1,0:T(8,128)} %copy-done.1, f32[1536]{0:T(1024)S(1)} %copy-done.10, f32[1536]{0:T(1024)S(1)} %copy-done.8, f32[256,768]{1,0:T(8,128)} %get-tuple-element.5, f32[768]{0:T(1024)S(1)} %convert_element_type.59), kind=kOutput, calls=%fused_computation.10 | convolution fusion | flops 606535680 | bytes 6306816 | tf_op jit(solution)/shard_map/dot_general | solution.py:34
  335.9 2.3 gather_fusion.2
  338.3 0.2 fusion.37
  338.5 3.1 fusion.18
  341.7 4.1 %fusion.3 = f32[256,1536]{1,0:T(8,128)} fusion(f32[256,1536]{1,0:T(8,128)} %copy-done.1, f32[256,1536]{1,0:T(8,128)} %fusion.18, f32[256]{0:T(256)S(1)} %fusion.37, f32[256,256]{1,0:T(8,128)S(1)} %copy-done.7, f32[256]{0:T(256)S(1)} %gather_fusion.2), kind=kOutput, calls=%fused_computation.7 | convolution fusion | flops 204537856 | bytes 4982784 | tf_op jit(solution)/shard_map/dot_general | solution.py:38
  (12 shorter events, 0.0 us)
Async XLA Ops:
  6.5 3.2 copy-start
  6.6 104.3 %all-reduce.14.cloned.1.call-start = ((), (), s32[]{:S(2)}) async-start(), calls=%async_computation.2 | async-start | bytes 2097152 | tf_op jit(solution)/shard_map/psum | solution.py:28
  6.6 3.2 copy-start.3
  9.7 1.9 copy-start.9
  9.7 1.9 copy-start.4
  9.7 1.9 copy-start.8
  11.5 210.6 %all-reduce.12.cloned.1.call-start = ((), (), s32[]{:S(2)}) async-start(), calls=%async_computation.1 | async-start | bytes 2097152 | tf_op jit(solution)/shard_map/psum | solution.py:28
  11.6 102.9 %copy-start.10 = (f32[1536]{0:T(1024)S(1)}, f32[1536]{0:T(1024)}, u32[]{:S(2)}) copy-start(f32[1536]{0:T(1024)} %param.7) | copy-start | bytes 18436
  114.6 3.7 %copy-start.5 = (f32[256,256]{1,0:T(8,128)S(1)}, f32[256,256]{1,0:T(8,128)}, u32[]{:S(2)}) copy-start(f32[256,256]{1,0:T(8,128)} %get-tuple-element.10) | copy-start | bytes 786436
  124.4 1.7 copy-start.2
  127.3 205.0 %all-reduce.10.cloned.1.call-start = ((), (), s32[]{:S(2)}) async-start(), calls=%async_computation | async-start | bytes 2097152 | tf_op jit(solution)/shard_map/psum | solution.py:28
  222.1 3.7 %copy-start.6 = (f32[256,256]{1,0:T(8,128)S(1)}, f32[256,256]{1,0:T(8,128)}, u32[]{:S(2)}) copy-start(f32[256,256]{1,0:T(8,128)} %get-tuple-element.8) | copy-start | bytes 786436
  234.5 1.7 copy-start.1
  332.3 3.7 %copy-start.7 = (f32[256,256]{1,0:T(8,128)S(1)}, f32[256,256]{1,0:T(8,128)}, u32[]{:S(2)}) copy-start(f32[256,256]{1,0:T(8,128)} %get-tuple-element.6) | copy-start | bytes 786436
Sparse Core Ops, SparseCore 0:
  11.6 99.1 all-reduce.13
  127.4 94.6 all-reduce.11
  237.5 94.7 all-reduce.9
where the time goes:
time: 353 us; the launch traced here: 352 us
  blocking collectives  145 us (41%)
  waiting for transfers between devices  139 us (39%)
  matrix products  46.3 us (13%)
  between operations  13.3 us (4%)
  local copies, waits for them, and re-layouts  7.3 us (2%)
    psum x3, blocking collectives, local_run(): lax.psum(jnp.dot(centred.astype(jnp.bfloat16), low_factor, preferred_elem...  145 us
    psum x3, waiting for transfers between devices, local_run(): lax.psum(lax.dot_general(part_bf, data_mat, DIMS_NT, preferred_element_ty...  139 us
    dot_general x3, matrix products, local_run(): jnp.dot(residual.astype(jnp.bfloat16), data_mat, preferred_element_type=j...  11 us
    dot_general x3, matrix products, local_run(): pulled = jnp.dot(kern_bf, part_bf, preferred_element_type=jnp.float32)  10 us
    dot_general x3, matrix products, local_run(): jnp.dot(kern_bf, log_grad.astype(jnp.bfloat16), preferred_element_type=jn...  9.43 us
    gather x3, local copies, waits for them, and re-layouts, local_run(): sq_norm = jnp.diagonal(gram_mat)  7.25 us
  transfers between devices with their start and end apart: 3, of which 3 were waited for; matrix products, arithmetic and copies ran while one was open for 2% of the time, Pallas kernels for 0%

commit v1 on v0

v1 whole, which is shorter than its diff:
```python
import functools
import math

import jax
import jax.numpy as jnp
from jax import lax
from jax.experimental import pallas as pl
from jax.experimental.pallas import tpu as pltpu
from jax.sharding import PartitionSpec as P

NUM_STEPS = 3
LANES = 128
NT = (((1,), (1,)), ((), ()))
NN = (((1,), (0,)), ((), ()))
F32 = jnp.float32
BF16 = jnp.bfloat16
MESH = pl.DeviceIdType.MESH


def _dot(a, b, dims):
    return lax.dot_general(a, b, dims, preferred_element_type=F32)


def _remote(src, dst, send, recv, device):
    return pltpu.make_async_remote_copy(
        src_ref=src, dst_ref=dst, send_sem=send, recv_sem=recv,
        device_id={"feat": device}, device_id_type=MESH,
    )


def _kernel(cfg, th_h, lam_h, u_h, mu_h, a_h, y_h, out_h,
            th, lam, u, mu, a, y, tb, xb, kb, p0, p1, d0, d1, r0, r1, ra, rb, gf,
            in_sem, out_sem, dd_s, dd_r, rs_s, rs_r, ag_s, ag_r, gg_s, gg_r, fw_s, fw_r):
    side, cut, blk, band, step, beta = cfg
    n, fl = th.shape
    m = a.shape[0]
    rest = m - cut
    chips = side * side
    own = n // chips

    me = lax.axis_index("feat")
    core = lax.rem(me, 2)
    chip = me // 2
    px, py = lax.rem(chip, side), chip // side
    partner = chip * 2 + (1 - core)
    hops = sorted(
        [(dx, dy) for dx in range(side) for dy in range(side) if (dx, dy) != (0, 0)],
        key=lambda t: -(min(t[0], side - t[0]) + min(t[1], side - t[1])),
    )

    def chip_at(dx, dy):
        return lax.rem(py + dy, side) * side + lax.rem(px + dx, side)

    to = [chip_at(dx, dy) for dx, dy in hops]
    frm = [chip_at(side - dx, side - dy) for dx, dy in hops]

    def rows(q):
        return pl.ds(pl.multiple_of(q * own, own), own)

    loads = [
        pltpu.make_async_copy(s, t, in_sem.at[i])
        for i, (s, t) in enumerate([(th_h, th), (mu_h, mu), (a_h, a), (u_h, u), (lam_h, lam), (y_h, y)])
    ]
    for cp in loads:
        cp.start()
    barrier = pltpu.get_barrier_semaphore()
    pl.semaphore_signal(barrier, 1, device_id={"feat": partner}, device_id_type=MESH)
    for q in to:
        pl.semaphore_signal(barrier, 1, device_id={"feat": q * 2 + core}, device_id_type=MESH)
    loads[0].wait()
    loads[1].wait()
    for j in range(0, fl, blk):
        t = th[:, j:j + blk]
        tb[:, j:j + blk] = t.astype(BF16)
        xb[:, j:j + blk] = (t - mu[:, j:j + blk]).astype(BF16)
    for cp in loads[2:]:
        cp.wait()
    pl.semaphore_wait(barrier, len(hops) + 1)

    def part0():
        for j in range(0, cut, 256):
            p0[:, j:j + 256] = _dot(tb[...], a[j:j + 256, :], NT)

    def part1():
        p1[:, 0:rest] = _dot(tb[...], a[cut:m, :], NT)
        p1[:, rest:rest + n] = _dot(tb[...], tb[...], NT)
        p1[:, rest + n:] = _dot(xb[...], u[...], NN)

    def reduce_rows(p, d, r):
        for k, q in enumerate(to):
            p[rows(q), :] = p[rows(q), :] + d[rows(q), :]
            _remote(p.at[rows(q), :], r.at[k], rs_s, rs_r.at[k], q * 2 + core).start()
        total = p[rows(chip), :] + d[rows(chip), :]
        for k in reversed(range(len(hops))):
            _remote(r.at[k], r.at[k], rs_s, rs_r.at[k], partner).wait_recv()
            total = total + r[k]
        return total

    def gather(buf, send, recv):
        for k, q in enumerate(to):
            _remote(buf.at[rows(chip), :], buf.at[rows(chip), :], send, recv.at[k], q * 2 + core).start()

    def forward(buf, recv, fs, fr):
        _remote(buf.at[rows(chip), :], buf.at[rows(chip), :], fs, fr, partner).start()
        for k in reversed(range(len(hops))):
            blk_ref = buf.at[rows(frm[k]), :]
            _remote(blk_ref, blk_ref, fs, recv.at[k], partner).wait_recv()
            _remote(blk_ref, blk_ref, fs, fr, partner).start()

    def drain(ref, send, count):
        part = ref.at[pl.ds(0, count * own), :]
        _remote(part, part, send, send, partner).wait_send()

    def one_step(s, carry):
        @pl.when(core == 0)
        def _():
            part1()
            out = _remote(p1, d1, dd_s, dd_r, partner)
            out.start()
            part0()
            _remote(p0, d0, dd_s, dd_r, partner).wait_recv()
            total = reduce_rows(p0, d0, r0)
            ra[rows(chip), :] = (y[:, 0:cut].astype(F32) - jax.nn.sigmoid(total)).astype(BF16)
            gather(ra, ag_s, ag_r)
            forward(ra, ag_r, fw_s.at[0], fw_r.at[0])
            _remote(rb, rb, fw_s.at[0], fw_r.at[0], partner).wait_recv()
            _remote(gf, gf, fw_s.at[1], fw_r.at[1], partner).wait_recv()
            out.wait_send()
            drain(p0, rs_s, len(hops))
            drain(ra, ag_s, len(hops))
            drain(ra, fw_s.at[0], chips)

        @pl.when(core == 1)
        def _():
            part0()
            out = _remote(p0, d0, dd_s, dd_r, partner)
            out.start()
            part1()
            _remote(p1, d1, dd_s, dd_r, partner).wait_recv()
            total = reduce_rows(p1, d1, r1)
            rb[rows(chip), 0:rest] = (y[:, cut:m].astype(F32) - jax.nn.sigmoid(total[:, 0:rest])).astype(BF16)
            rb[rows(chip), rest:] = total[:, rest + n:].astype(BF16)
            gf[rows(chip), :] = total[:, rest:rest + n]
            gather(rb, ag_s, ag_r)
            gather(gf, gg_s, gg_r)
            forward(rb, ag_r, fw_s.at[0], fw_r.at[0])
            forward(gf, gg_r, fw_s.at[1], fw_r.at[1])
            _remote(ra, ra, fw_s.at[0], fw_r.at[0], partner).wait_recv()
            out.wait_send()
            drain(p1, rs_s, len(hops))
            drain(rb, ag_s, len(hops))
            drain(gf, gg_s, len(hops))
            drain(rb, fw_s.at[0], chips)
            drain(gf, fw_s.at[1], chips)

        g = gf[...]
        eye = lax.broadcasted_iota(jnp.int32, (n, n), 0) == lax.broadcasted_iota(jnp.int32, (n, n), 1)
        diag = jnp.where(eye, g, 0.0)
        dist = jnp.maximum(
            jnp.sum(diag, axis=1, keepdims=True) + jnp.sum(diag, axis=0, keepdims=True) - 2.0 * g, 0.0)
        kern = jnp.exp(-dist / band)
        ksum = jnp.sum(kern, axis=1, keepdims=True)
        kb[...] = kern.astype(BF16)
        for j in range(0, fl, blk):
            c = slice(j, j + blk)
            t = th[:, c]
            lik = _dot(ra[...], a[0:cut, c], NN) + _dot(rb[:, 0:rest], a[cut:m, c], NN)
            low = _dot(rb[:, rest:], u[c, :], NT)
            score = beta * lik - (t - mu[:, c]) * lam[:, c] - low
            drive = _dot(kb[...], score.astype(BF16), NN)
            pull = _dot(kb[...], tb[:, c], NN)
            t = t + step * ((drive + (2.0 / band) * (ksum * t - pull)) / n)
            th[:, c] = t
            tb[:, c] = t.astype(BF16)
            xb[:, c] = (t - mu[:, c]).astype(BF16)
        return carry

    lax.fori_loop(0, NUM_STEPS, one_step, 0)
    done = pltpu.make_async_copy(th, out_h, out_sem)
    done.start()
    done.wait()


def solution(mesh):
    feat = mesh.shape["feat"]
    side = math.isqrt(feat // 2)

    def local_run(particles, prec_diag, low_factor, prior_mean, data_mat, labels):
        n, fl = particles.shape
        m = data_mat.shape[0]
        rank = low_factor.shape[1]
        dim = fl * feat
        chips = side * side
        own = n // chips
        cut = 2 * m // 3
        wide = m - cut + n + rank
        cfg = (side, cut, 256, 2.0 * dim, dim / 4.0, 2.0 / math.sqrt(m * dim))
        peers = chips - 1
        dma = pltpu.SemaphoreType.DMA
        return pl.pallas_call(
            functools.partial(_kernel, cfg),
            out_shape=jax.ShapeDtypeStruct((n, fl), F32),
            in_specs=[pl.BlockSpec(memory_space=pl.ANY)] * 6,
            out_specs=pl.BlockSpec(memory_space=pl.ANY),
            scratch_shapes=[
                pltpu.VMEM((n, fl), F32), pltpu.VMEM((1, fl), F32), pltpu.VMEM((fl, rank), BF16),
                pltpu.VMEM((1, fl), F32), pltpu.VMEM((m, fl), BF16), pltpu.VMEM((1, m), jnp.int32),
                pltpu.VMEM((n, fl), BF16), pltpu.VMEM((n, fl), BF16), pltpu.VMEM((n, n), BF16),
                pltpu.VMEM((n, cut), F32), pltpu.VMEM((n, wide), F32),
                pltpu.VMEM((n, cut), F32), pltpu.VMEM((n, wide), F32),
                pltpu.VMEM((peers, own, cut), F32), pltpu.VMEM((peers, own, wide), F32),
                pltpu.VMEM((n, cut), BF16), pltpu.VMEM((n, m - cut + rank), BF16), pltpu.VMEM((n, n), F32),
                dma((6,)), dma, dma, dma, dma, dma((peers,)), dma, dma((peers,)), dma, dma((peers,)),
                dma((2,)), dma((2,)),
            ],
            compiler_params=pltpu.CompilerParams(
                collective_id=0, has_side_effects=True, vmem_limit_bytes=60 * 1024 * 1024),
        )(particles, prec_diag.reshape(1, fl), low_factor, prior_mean.reshape(1, fl), data_mat,
          labels.reshape(1, m))

    return jax.shard_map(
        local_run,
        mesh=mesh,
        in_specs=(P("ens", "feat"), P(("ens", "feat")), P(("ens", "feat"), None),
                  P(("ens", "feat")), P("ens", "feat"), P("ens")),
        out_specs=P("ens", "feat"),
        check_vma=False,
    )
```

time: 353 us -> 83.1 us (0.24)
  blocking collectives: 145 us -> 0 us
  waiting for transfers between devices: 139 us -> 0 us
  Pallas kernels: 0 us -> 76.4 us
  matrix products: 46.3 us -> 0 us
  between operations: 13.3 us -> 0.01 us
    psum x3 -> x0, blocking collectives: 145 us -> none  [local_run(): lax.psum(jnp.dot(centred.astype(jnp.bfloat16), low_factor, preferred_elem...]
    psum x3 -> x0, waiting for transfers between devices: 139 us -> none  [local_run(): lax.psum(lax.dot_general(part_bf, data_mat, DIMS_NT, preferred_element_ty...]
    pallas_call x0 -> x1, Pallas kernels: none -> 76.4 us  [local_run(): pl.pallas_call(functools.partial(_kernel, cfg), out_shape=jax.ShapeDtypeS...]
    dot_general x18 -> x0, matrix products: 46.3 us -> none  [the longest x3 11 us: local_run(): jnp.dot(residual.astype(jnp.bfloat16), data_mat, preferred_element_type=j...]
    gather x3 -> x0, local copies, waits for them, and re-layouts: 7.25 us -> none  [local_run(): sq_norm = jnp.diagonal(gram_mat)]
    reshape x0 -> x3, local copies, waits for them, and re-layouts: none -> 3.85 us  [the longest x1 1.29 us: local_run(): prec_diag.reshape(1, fl)]
  transfers between devices with their start and end apart: 3 -> 0, of which waited for: 3 -> 0; matrix products, arithmetic and copies ran while one was open for 2% -> 0% of each run, Pallas kernels for 0% -> 0%
where the time goes in v1:
time: 83.1 us; the launch traced here: 82.9 us
  Pallas kernels  76.4 us (92%)
  local copies, waits for them, and re-layouts  6.51 us (8%)
    pallas_call x1, Pallas kernels, local_run(): pl.pallas_call(functools.partial(_kernel, cfg), out_shape=jax.ShapeDtypeS...  76.4 us
    unnamed x1, local copies, waits for them, and re-layouts  2.66 us

profile of v1, /device:TPU:97, one launch (start us, length us, event | category | flops | bytes accessed | tf_op | source)
XLA Modules:
  0.0 82.9 jit_solution(3770103674672206635)
XLA Ops:
  0.0 1.3 %reshape.11.y_h = s32[1,768]{1,0:T(1,128)} reshape(s32[768]{0:T(1024)} %param.11) | data formatting | bytes 6144 | tf_op jit(solution)/shard_map/reshape | solution.py:219
  1.3 1.3 %reshape.9.lam_h = f32[1,1536]{1,0:T(1,128)} reshape(f32[1536]{0:T(1024)} %param.7) | data formatting | bytes 12288 | tf_op jit(solution)/shard_map/reshape | solution.py:218
  2.6 1.3 %reshape.10.mu_h = f32[1,1536]{1,0:T(1,128)} reshape(f32[1536]{0:T(1024)} %param.9) | data formatting | bytes 12288 | tf_op jit(solution)/shard_map/reshape | solution.py:218
  3.9 76.4 %shard_map.64 = f32[256,1536]{1,0:T(8,128)} custom-call(f32[256,1536]{1,0:T(8,128)} %th_h.1, f32[1,1536]{1,0:T(1,128)} %reshape.9.lam_h, bf16[1536,128]{1,0:T(8,128)(2,1)} %u_h.1, f32[1,1536]{1,0:T(1,128)} %reshape.10.mu_h, bf16[768,1536]{1,0:T(8,128)(2,1)} %a_h.1, s32[1,768]{1,0:T(1,128)} %reshape.11.y_h), custom_call_target="tpu_custom_call" | custom-call | tf_op jit(solution)/shard_map/pallas_call | solution.py:200
  80.2 2.7 %copy.8 = f32[256,1536]{1,0:T(8,128)} copy(f32[256,1536]{1,0:T(8,128)} %shard_map.64) | data formatting | bytes 3145728

commit v2 on v0

v2 whole, which is shorter than its diff:
```python
import functools
import math

import jax
import jax.numpy as jnp
from jax import lax
from jax.experimental import pallas as pl
from jax.experimental.pallas import tpu as pltpu
from jax.sharding import PartitionSpec as P

NUM_STEPS = 3
HALF = 128
NT = (((1,), (1,)), ((), ()))
NN = (((1,), (0,)), ((), ()))
F32 = jnp.float32
BF16 = jnp.bfloat16
MESH = pl.DeviceIdType.MESH


def _dot(a, b, dims):
    return lax.dot_general(a, b, dims, preferred_element_type=F32)


def _remote(src, dst, send, recv, device):
    return pltpu.make_async_remote_copy(
        src_ref=src, dst_ref=dst, send_sem=send, recv_sem=recv,
        device_id={"feat": device}, device_id_type=MESH,
    )


CHUNKS = ((("z", 0, 256), ("z", 256, 256)), (("gq",), ("z", 512, 256)))


def _kernel(cfg, th_h, lam_h, u_h, mu_h, a_h, y_h, out_h,
            th, lam, u, mu, a, y, tb, xb, kb, ps, parts, others, slots, rz, gg, qb,
            in_sem, out_sem, dd_s, dd_r, rs_s, rs_r, ag_s, ag_r, fw_s, fw_r):
    side, blk, band, step, beta = cfg
    n, fl = th.shape
    chips = side * side
    own = n // chips

    me = lax.axis_index("feat")
    core = lax.rem(me, 2)
    chip = me // 2
    px, py = lax.rem(chip, side), chip // side
    partner = chip * 2 + (1 - core)
    hops = sorted(
        [(dx, dy) for dx in range(side) for dy in range(side) if (dx, dy) != (0, 0)],
        key=lambda t: -(min(t[0], side - t[0]) + min(t[1], side - t[1])),
    )
    peers = len(hops)

    def chip_at(dx, dy):
        return lax.rem(py + dy, side) * side + lax.rem(px + dx, side)

    to = [chip_at(dx, dy) for dx, dy in hops]
    frm = [chip_at(side - dx, side - dy) for dx, dy in hops]

    def rows(q, height):
        return pl.ds(pl.multiple_of(q * height, height), height)

    ids = {ch: i for i, ch in enumerate(CHUNKS[0] + CHUNKS[1])}
    zcols = {ch: i for i, ch in enumerate(c for c in ids if c[0] == "z")}
    n_z = len(zcols)

    def items(ch):
        if ch[0] == "z":
            return [(rz[zcols[ch]], own, zcols[ch])]
        return [(gg, own + own // 2, n_z), (qb, own, n_z + 1)]

    loads = [
        pltpu.make_async_copy(s, t, in_sem.at[i])
        for i, (s, t) in enumerate([(th_h, th), (mu_h, mu), (u_h, u), (a_h, a), (lam_h, lam), (y_h, y)])
    ]
    for cp in loads:
        cp.start()
    barrier = pltpu.get_barrier_semaphore()
    pl.semaphore_signal(barrier, 1, device_id={"feat": partner}, device_id_type=MESH)
    for q in to:
        pl.semaphore_signal(barrier, 1, device_id={"feat": q * 2 + core}, device_id_type=MESH)
    loads[0].wait()
    loads[1].wait()

    def row(ref, c):
        return ref[c].reshape(1, c.stop - c.start)

    blocks = [slice(j, j + blk) for j in range(0, fl, blk)]
    for c in blocks:
        t = th[:, c]
        tb[:, c] = t.astype(BF16)
        xb[:, c] = (t - row(mu, c)).astype(BF16)
    for cp in loads[2:]:
        cp.wait()

    def partial(ch):
        p = parts[ids[ch]]
        if ch[0] == "z":
            p[...] = _dot(tb[...], a[ch[1]:ch[1] + ch[2], :], NT)
            return
        g = _dot(tb[...], tb[...], NT)
        q = _dot(xb[...], u[...], NN)
        tall = 2 * own + own // 2
        for i in range(chips):
            o = i * tall
            p[o:o + own, :] = g[i * own:(i + 1) * own, HALF:]
            p[o + own:o + 2 * own, :] = q[i * own:(i + 1) * own, :]
            p[o + 2 * own:o + tall, :] = g[i * own // 2:(i + 1) * own // 2, :HALF]

    def height(ch):
        return own if ch[0] == "z" else 2 * own + own // 2

    def scatter(ch):
        i = ids[ch]
        p, d, r, h = parts[i], others[i], slots[i], height(ch)
        _remote(p, d, dd_s.at[i], dd_r.at[i], partner).wait_recv()
        for k, q in enumerate(to):
            p[rows(q, h), :] = p[rows(q, h), :] + d[rows(q, h), :]
            _remote(p.at[rows(q, h), :], r.at[k], rs_s.at[i], rs_r.at[i, k], q * 2 + core).start()

    def complete(ch):
        i = ids[ch]
        p, d, r, h = parts[i], others[i], slots[i], height(ch)
        total = p[rows(chip, h), :] + d[rows(chip, h), :]
        for k in reversed(range(peers)):
            _remote(r.at[k], r.at[k], rs_s.at[i], rs_r.at[i, k], partner).wait_recv()
            total = total + r[k]
        if ch[0] == "z":
            c = slice(ch[1], ch[1] + ch[2])
            rz[zcols[ch]][rows(chip, own), :] = (row(y, c).astype(F32) - jax.nn.sigmoid(total)).astype(BF16)
        else:
            qb[rows(chip, own), :] = total[own:2 * own, :].astype(BF16)
            gg[rows(chip, own + own // 2), :] = jnp.concatenate([total[:own], total[2 * own:]], axis=0)
        for buf, h, j in items(ch):
            mine = buf.at[rows(chip, h), :]
            for k, q in enumerate(to):
                _remote(mine, mine, ag_s.at[j], ag_r.at[j, k], q * 2 + core).start()
            _remote(mine, mine, fw_s.at[j], fw_r.at[j], partner).start()

    def forward(ch):
        for k in reversed(range(peers)):
            for buf, h, j in items(ch):
                piece = buf.at[rows(frm[k], h), :]
                _remote(piece, piece, fw_s.at[j], ag_r.at[j, k], partner).wait_recv()
                _remote(piece, piece, fw_s.at[j], fw_r.at[j], partner).start()

    def forwarded(ch):
        for buf, h, j in items(ch):
            _remote(buf, buf, fw_s.at[j], fw_r.at[j], partner).wait_recv()

    def drain(ch_own, ch_other):
        for ch in ch_other:
            i = ids[ch]
            _remote(parts[i], parts[i], dd_s.at[i], dd_r.at[i], partner).wait_send()
        for ch in ch_own:
            i, h = ids[ch], height(ch)
            part = parts[i].at[pl.ds(0, peers * h), :]
            _remote(part, part, rs_s.at[i], dd_r.at[i], partner).wait_send()
            for buf, h, j in items(ch):
                part = buf.at[pl.ds(0, peers * h), :]
                _remote(part, part, ag_s.at[j], fw_r.at[j], partner).wait_send()
                _remote(buf, buf, fw_s.at[j], fw_r.at[j], partner).wait_send()

    def kernel_matrix():
        h = own + own // 2
        g1 = jnp.concatenate([gg[i * h:i * h + own, :] for i in range(chips)], axis=0)
        g00 = jnp.concatenate([gg[i * h + own:(i + 1) * h, :] for i in range(chips)], axis=0)
        g01, g11 = g1[:HALF], g1[HALF:]
        eye = (lax.broadcasted_iota(jnp.int32, (HALF, HALF), 0)
               == lax.broadcasted_iota(jnp.int32, (HALF, HALF), 1))
        e0, e1 = jnp.where(eye, g00, 0.0), jnp.where(eye, g11, 0.0)
        c0, c1 = jnp.sum(e0, axis=1, keepdims=True), jnp.sum(e1, axis=1, keepdims=True)
        r0, r1 = jnp.sum(e0, axis=0, keepdims=True), jnp.sum(e1, axis=0, keepdims=True)
        k00 = jnp.exp(-jnp.maximum(c0 + r0 - 2.0 * g00, 0.0) / band)
        k01 = jnp.exp(-jnp.maximum(c0 + r1 - 2.0 * g01, 0.0) / band)
        k11 = jnp.exp(-jnp.maximum(c1 + r1 - 2.0 * g11, 0.0) / band)
        k10 = k01.T
        kb[:HALF, :HALF] = k00.astype(BF16)
        kb[:HALF, HALF:] = k01.astype(BF16)
        kb[HALF:, :HALF] = k10.astype(BF16)
        kb[HALF:, HALF:] = k11.astype(BF16)
        return jnp.concatenate([jnp.sum(k00, axis=1, keepdims=True) + jnp.sum(k01, axis=1, keepdims=True),
                                jnp.sum(k10, axis=1, keepdims=True) + jnp.sum(k11, axis=1, keepdims=True)], axis=0)

    def lik(ch, c):
        return _dot(rz[zcols[ch]][...], a[ch[1]:ch[1] + ch[2], c], NN)

    def one_step(s, role):
        mine, other = CHUNKS[role], CHUNKS[1 - role]
        for idx, ch in enumerate(other):
            partial(ch)
            if idx == 0:
                @pl.when(s == 0)
                def _():
                    pl.semaphore_wait(barrier, peers + 1)
            i = ids[ch]
            _remote(parts[i], others[i], dd_s.at[i], dd_r.at[i], partner).start()
        for ch in mine:
            partial(ch)
        for ch in mine:
            scatter(ch)
        for ch in mine:
            complete(ch)
        forward(mine[0])
        forwarded(other[0])
        ksum = kernel_matrix()
        for c in blocks:
            t = th[:, c]
            early = _dot(qb[...], u[c, :], NT)
            for ch in (mine[0], other[0]):
                if ch[0] == "z":
                    ps[:, c] = beta * lik(ch, c) - (t - row(mu, c)) * row(lam, c) - early
            th[:, c] = t + (step * 2.0 / (band * n)) * (ksum * t - _dot(kb[...], tb[:, c], NN))
        for ch, ch2 in zip(mine[1:], other[1:]):
            forward(ch)
            for c in blocks:
                ps[:, c] = ps[:, c] + beta * lik(ch, c)
            forwarded(ch2)
            for c in blocks:
                score = ps[:, c] + beta * lik(ch2, c)
                if ch != mine[-1]:
                    ps[:, c] = score
                    continue
                t = th[:, c] + (step / n) * _dot(kb[...], score.astype(BF16), NN)
                th[:, c] = t
                tb[:, c] = t.astype(BF16)
                xb[:, c] = (t - row(mu, c)).astype(BF16)
        drain(mine, other)

    for role in range(2):
        @pl.when(core == role)
        def _():
            def body(s, carry):
                one_step(s, role)
                return carry
            lax.fori_loop(0, NUM_STEPS, body, 0)

    done = pltpu.make_async_copy(th, out_h, out_sem)
    done.start()
    done.wait()


def solution(mesh):
    feat = mesh.shape["feat"]
    side = math.isqrt(feat // 2)

    def local_run(particles, prec_diag, low_factor, prior_mean, data_mat, labels):
        n, fl = particles.shape
        m = data_mat.shape[0]
        rank = low_factor.shape[1]
        dim = fl * feat
        chips = side * side
        own = n // chips
        peers = chips - 1
        cfg = (side, 256, 2.0 * dim, dim / 4.0, 2.0 / math.sqrt(m * dim))
        dma = pltpu.SemaphoreType.DMA
        every = CHUNKS[0] + CHUNKS[1]
        tall = 2 * own + own // 2
        shape = [(n, ch[2]) if ch[0] == "z" else (chips * tall, HALF) for ch in every]
        slot = [(peers, own, ch[2]) if ch[0] == "z" else (peers, tall, HALF) for ch in every]
        n_items = len(every) + 1
        return pl.pallas_call(
            functools.partial(_kernel, cfg),
            out_shape=jax.ShapeDtypeStruct((n, fl), F32),
            in_specs=[pl.BlockSpec(memory_space=pl.ANY)] * 6,
            out_specs=pl.BlockSpec(memory_space=pl.ANY),
            scratch_shapes=[
                pltpu.VMEM((n, fl), F32), pltpu.VMEM((fl,), F32), pltpu.VMEM((fl, rank), BF16),
                pltpu.VMEM((fl,), F32), pltpu.VMEM((m, fl), BF16), pltpu.VMEM((m,), jnp.int32),
                pltpu.VMEM((n, fl), BF16), pltpu.VMEM((n, fl), BF16), pltpu.VMEM((n, n), BF16),
                pltpu.VMEM((n, fl), F32),
                [pltpu.VMEM(s, F32) for s in shape], [pltpu.VMEM(s, F32) for s in shape],
                [pltpu.VMEM(s, F32) for s in slot],
                [pltpu.VMEM((n, ch[2]), BF16) for ch in every if ch[0] == "z"],
                pltpu.VMEM((chips * (own + own // 2), HALF), F32), pltpu.VMEM((n, rank), BF16),
                dma((6,)), dma, dma((len(every),)), dma((len(every),)),
                dma((len(every),)), dma((len(every), peers)),
                dma((n_items,)), dma((n_items, peers)), dma((n_items,)), dma((n_items,)),
            ],
            compiler_params=pltpu.CompilerParams(
                collective_id=0, has_side_effects=True, vmem_limit_bytes=60 * 1024 * 1024),
        )(particles, prec_diag, low_factor, prior_mean, data_mat, labels)

    return jax.shard_map(
        local_run,
        mesh=mesh,
        in_specs=(P("ens", "feat"), P(("ens", "feat")), P(("ens", "feat"), None),
                  P(("ens", "feat")), P("ens", "feat"), P("ens")),
        out_specs=P("ens", "feat"),
        check_vma=False,
    )
```

time: 353 us -> 73 us (0.21)
  blocking collectives: 145 us -> 0 us
  waiting for transfers between devices: 139 us -> 0 us
  Pallas kernels: 0 us -> 70.3 us
  matrix products: 46.3 us -> 0 us
  between operations: 13.3 us -> 0.01 us
  local copies, waits for them, and re-layouts: 7.3 us -> 2.66 us
    psum x3 -> x0, blocking collectives: 145 us -> none  [local_run(): lax.psum(jnp.dot(centred.astype(jnp.bfloat16), low_factor, preferred_elem...]
    psum x3 -> x0, waiting for transfers between devices: 139 us -> none  [local_run(): lax.psum(lax.dot_general(part_bf, data_mat, DIMS_NT, preferred_element_ty...]
    pallas_call x0 -> x1, Pallas kernels: none -> 70.3 us  [local_run(): pl.pallas_call(functools.partial(_kernel, cfg), out_shape=jax.ShapeDtypeS...]
    dot_general x18 -> x0, matrix products: 46.3 us -> none  [the longest x3 11 us: local_run(): jnp.dot(residual.astype(jnp.bfloat16), data_mat, preferred_element_type=j...]
    gather x3 -> x0, local copies, waits for them, and re-layouts: 7.25 us -> none  [local_run(): sq_norm = jnp.diagonal(gram_mat)]
  transfers between devices with their start and end apart: 3 -> 0, of which waited for: 3 -> 0; matrix products, arithmetic and copies ran while one was open for 2% -> 0% of each run, Pallas kernels for 0% -> 0%
where the time goes in v2:
time: 73 us; the launch traced here: 72.9 us
  Pallas kernels  70.3 us (96%)
  local copies, waits for them, and re-layouts  2.66 us (4%)
    pallas_call x1, Pallas kernels, local_run(): pl.pallas_call(functools.partial(_kernel, cfg), out_shape=jax.ShapeDtypeS...  70.3 us
    unnamed x1, local copies, waits for them, and re-layouts  2.66 us

profile of v2, /device:TPU:97, one launch (start us, length us, event | category | flops | bytes accessed | tf_op | source)
XLA Modules:
  0.0 72.9 jit_solution(17441832340348757747)
XLA Ops:
  0.0 70.3 %shard_map.64 = f32[256,1536]{1,0:T(8,128)} custom-call(f32[256,1536]{1,0:T(8,128)} %th_h.1, f32[1536]{0:T(1024)} %lam_h.1, bf16[1536,128]{1,0:T(8,128)(2,1)} %u_h.1, f32[1536]{0:T(1024)} %mu_h.1, bf16[768,1536]{1,0:T(8,128)(2,1)} %a_h.1, s32[768]{0:T(1024)} %y_h.1), custom_call_target="tpu_custom_call" | custom-call | tf_op jit(solution)/shard_map/pallas_call | solution.py:261
  70.3 2.7 %copy.8 = f32[256,1536]{1,0:T(8,128)} copy(f32[256,1536]{1,0:T(8,128)} %shard_map.64) | data formatting | bytes 3145728

commit v3 on v2

v3 whole, which is shorter than its diff:
```python
import functools
import math

import jax
import jax.numpy as jnp
from jax import lax
from jax.experimental import pallas as pl
from jax.experimental.pallas import tpu as pltpu
from jax.sharding import PartitionSpec as P

NUM_STEPS = 3
HALF = 128
NT = (((1,), (1,)), ((), ()))
NN = (((1,), (0,)), ((), ()))
F32 = jnp.float32
BF16 = jnp.bfloat16
MESH = pl.DeviceIdType.MESH


def _dot(a, b, dims):
    return lax.dot_general(a, b, dims, preferred_element_type=F32)


def _remote(src, dst, send, recv, device):
    return pltpu.make_async_remote_copy(
        src_ref=src, dst_ref=dst, send_sem=send, recv_sem=recv,
        device_id={"feat": device}, device_id_type=MESH,
    )


CHUNKS = (
    (("q",), ("z", 0, 256), ("z", 512, 128)),
    (("g",), ("z", 256, 256), ("z", 640, 128)),
)
DIRECT = tuple(chunks[-1] for chunks in CHUNKS)
EARLY = 512


def _kernel(cfg, th_h, lam_h, u_h, mu_h, a_h, y_h, out_v,
            th, lam, u, mu, a, y, at, tb, xb, kb, ps, parts, others, slots, rz, gg, qb,
            in_sem, dd_s, dd_r, rs_s, rs_r, ag_s, ag_r, fw_s, fw_r):
    side, blk, band, step, beta = cfg
    n, fl = th.shape
    chips = side * side
    own = n // chips

    me = lax.axis_index("feat")
    core = lax.rem(me, 2)
    chip = me // 2
    px, py = lax.rem(chip, side), chip // side
    partner = chip * 2 + (1 - core)
    hops = sorted(
        [(dx, dy) for dx in range(side) for dy in range(side) if (dx, dy) != (0, 0)],
        key=lambda t: -(min(t[0], side - t[0]) + min(t[1], side - t[1])),
    )
    peers = len(hops)

    def chip_at(dx, dy):
        return lax.rem(py + dy, side) * side + lax.rem(px + dx, side)

    to = [chip_at(dx, dy) for dx, dy in hops]
    frm = [chip_at(side - dx, side - dy) for dx, dy in hops]

    def rows(q, height):
        return pl.ds(pl.multiple_of(q * height, height), height)

    ids = {ch: i for i, ch in enumerate(CHUNKS[0] + CHUNKS[1])}

    def held(ch):
        if ch[0] == "z":
            return rz.at[:, ch[1]:ch[1] + ch[2]]
        return gg if ch[0] == "g" else qb

    def height(ch):
        return own + own // 2 if ch[0] == "g" else own

    loads = [
        pltpu.make_async_copy(s, t, in_sem.at[i])
        for i, (s, t) in enumerate([(th_h, th), (mu_h, mu), (u_h, u), (a_h, a), (lam_h, lam), (y_h, y)])
    ]
    for cp in loads:
        cp.start()
    barrier = pltpu.get_barrier_semaphore()
    pl.semaphore_signal(barrier, 1, device_id={"feat": partner}, device_id_type=MESH)
    for q in to:
        for c in range(2):
            pl.semaphore_signal(barrier, 1, device_id={"feat": q * 2 + c}, device_id_type=MESH)
    loads[0].wait()
    loads[1].wait()

    def row(ref, c):
        return ref[c].reshape(1, c.stop - c.start)

    blocks = [slice(j, j + blk) for j in range(0, fl, blk)]
    for c in blocks:
        t = th[:, c]
        tb[:, c] = t.astype(BF16)
        xb[:, c] = (t - row(mu, c)).astype(BF16)
    for cp in loads[2:]:
        cp.wait()
    z_at = {}
    for chunks in CHUNKS:
        for ch in chunks:
            if ch[0] == "z":
                z_at[ch] = sum(other[2] for other in z_at)
                for c in blocks:
                    for j in range(0, ch[2], HALF):
                        at[c, z_at[ch] + j:z_at[ch] + j + HALF] = a[ch[1] + j:ch[1] + j + HALF, c].T

    def partial_first(role):
        p = parts[ids[CHUNKS[role][0]]]
        if CHUNKS[role][0][0] == "q":
            p[...] = _dot(xb[...], u[...], NN)
            return
        g = _dot(tb[...], tb[...], NT)
        tall = own + own // 2
        for i in range(chips):
            o = i * tall
            p[o:o + own, :] = g[i * own:(i + 1) * own, HALF:]
            p[o + own:o + tall, :] = g[i * own // 2:(i + 1) * own // 2, :HALF]

    def partial_z(role):
        zs = CHUNKS[role][1:]
        start = z_at[zs[0]]
        width = sum(ch[2] for ch in zs)
        z = _dot(tb[...], at[:, start:start + width], NN)
        for ch in zs:
            o = z_at[ch] - start
            parts[ids[ch]][...] = z[:, o:o + ch[2]]

    def scatter(ch):
        i = ids[ch]
        p, d, r, h = parts[i], others[i], slots[i], height(ch)
        _remote(p, d, dd_s.at[i], dd_r.at[i], partner).wait_recv()
        for k, q in enumerate(to):
            p[rows(q, h), :] = p[rows(q, h), :] + d[rows(q, h), :]
            _remote(p.at[rows(q, h), :], r.at[k], rs_s.at[i], rs_r.at[i, k], q * 2 + core).start()

    def complete(ch):
        i = ids[ch]
        p, d, r, h = parts[i], others[i], slots[i], height(ch)
        total = p[rows(chip, h), :] + d[rows(chip, h), :]
        for k in reversed(range(peers)):
            _remote(r.at[k], r.at[k], rs_s.at[i], rs_r.at[i, k], partner).wait_recv()
            total = total + r[k]
        if ch[0] == "z":
            c = slice(ch[1], ch[1] + ch[2])
            done = (row(y, c).astype(F32) - jax.nn.sigmoid(total)).astype(BF16)
        else:
            done = total.astype(BF16) if ch[0] == "q" else total
        buf = held(ch)
        buf[rows(chip, h), :] = done
        mine = buf.at[rows(chip, h), :]
        for k, q in enumerate(to):
            _remote(mine, mine, ag_s.at[i], ag_r.at[i, k], q * 2 + core).start()
            if ch in DIRECT:
                _remote(mine, mine, fw_s.at[i], ag_r.at[i, k], q * 2 + 1 - core).start()
        _remote(mine, mine, fw_s.at[i], fw_r.at[i], partner).start()

    def forward(ch):
        i, buf, h = ids[ch], held(ch), height(ch)
        for k in reversed(range(peers)):
            piece = buf.at[rows(frm[k], h), :]
            _remote(piece, piece, fw_s.at[i], ag_r.at[i, k], partner).wait_recv()
            _remote(piece, piece, fw_s.at[i], fw_r.at[i], partner).start()

    def direct(ch, role):
        i, buf, h = ids[ch], held(ch), height(ch)
        for k in reversed(range(peers)):
            piece = buf.at[rows(frm[k], h), :]
            _remote(piece, piece, fw_s.at[i], ag_r.at[i, k], partner).wait_recv()
        if ch not in CHUNKS[role]:
            piece = buf.at[rows(chip, h), :]
            _remote(piece, piece, fw_s.at[i], fw_r.at[i], partner).wait_recv()

    def forwarded(ch):
        i, buf = ids[ch], held(ch)
        _remote(buf, buf, fw_s.at[i], fw_r.at[i], partner).wait_recv()

    def drain(ch_own, ch_other):
        for ch in ch_other:
            i = ids[ch]
            _remote(parts[i], parts[i], dd_s.at[i], dd_r.at[i], partner).wait_send()
        for ch in ch_own:
            i, h, buf = ids[ch], height(ch), held(ch)
            part = parts[i].at[pl.ds(0, peers * h), :]
            _remote(part, part, rs_s.at[i], dd_r.at[i], partner).wait_send()
            part = buf.at[pl.ds(0, peers * h), :]
            _remote(part, part, ag_s.at[i], fw_r.at[i], partner).wait_send()
            _remote(buf, buf, fw_s.at[i], fw_r.at[i], partner).wait_send()

    def kernel_matrix():
        h = own + own // 2
        g1 = jnp.concatenate([gg[i * h:i * h + own, :] for i in range(chips)], axis=0)
        g00 = jnp.concatenate([gg[i * h + own:(i + 1) * h, :] for i in range(chips)], axis=0)
        g01, g11 = g1[:HALF], g1[HALF:]
        eye = (lax.broadcasted_iota(jnp.int32, (HALF, HALF), 0)
               == lax.broadcasted_iota(jnp.int32, (HALF, HALF), 1))
        e0, e1 = jnp.where(eye, g00, 0.0), jnp.where(eye, g11, 0.0)
        c0, c1 = jnp.sum(e0, axis=1, keepdims=True), jnp.sum(e1, axis=1, keepdims=True)
        r0, r1 = jnp.sum(e0, axis=0, keepdims=True), jnp.sum(e1, axis=0, keepdims=True)
        k00 = jnp.exp(-jnp.maximum(c0 + r0 - 2.0 * g00, 0.0) / band)
        k01 = jnp.exp(-jnp.maximum(c0 + r1 - 2.0 * g01, 0.0) / band)
        k11 = jnp.exp(-jnp.maximum(c1 + r1 - 2.0 * g11, 0.0) / band)
        k10 = k01.T
        kb[:HALF, :HALF] = k00.astype(BF16)
        kb[:HALF, HALF:] = k01.astype(BF16)
        kb[HALF:, :HALF] = k10.astype(BF16)
        kb[HALF:, HALF:] = k11.astype(BF16)
        return jnp.concatenate([jnp.sum(k00, axis=1, keepdims=True) + jnp.sum(k01, axis=1, keepdims=True),
                                jnp.sum(k10, axis=1, keepdims=True) + jnp.sum(k11, axis=1, keepdims=True)], axis=0)

    def swap(chs):
        for ch in chs:
            i = ids[ch]
            _remote(parts[i], others[i], dd_s.at[i], dd_r.at[i], partner).start()

    def one_step(role, last):
        mine, other = CHUNKS[role], CHUNKS[1 - role]

        for ch in mine:
            with jax.named_scope(f"scatter_{ch[0]}{ids[ch]}"):
                scatter(ch)
        for ch in mine:
            with jax.named_scope(f"complete_{ch[0]}{ids[ch]}"):
                complete(ch)
        with jax.named_scope("forward0"):
            forward(mine[0])
        with jax.named_scope("forwarded0"):
            forwarded(other[0])
        with jax.named_scope("base"):
            ksum = kernel_matrix()
            for c in blocks:
                t = th[:, c]
                ps[:, c] = (t - row(mu, c)) * row(lam, c) + _dot(qb[...], u[c, :], NT)
                th[:, c] = t + (step * 2.0 / (band * n)) * (ksum * t - _dot(kb[...], tb[:, c], NN))
        with jax.named_scope("forward1"):
            forward(mine[1])
        with jax.named_scope("forwarded1"):
            forwarded(other[1])
        with jax.named_scope("early"):
            for c in blocks:
                ps[:, c] = beta * _dot(rz[:, :EARLY], a[:EARLY, c], NN) - ps[:, c]
        with jax.named_scope("direct"):
            direct(mine[2], role)
            direct(other[2], role)
        with jax.named_scope("drain"):
            drain(mine, other)
        with jax.named_scope("update"):
            for c in blocks:
                score = ps[:, c] + beta * _dot(rz[:, EARLY:], a[EARLY:, c], NN)
                t = th[:, c] + (step / n) * _dot(kb[...], score.astype(BF16), NN)
                if last:
                    out_v[:, c] = t
                    continue
                th[:, c] = t
                tb[:, c] = t.astype(BF16)
                xb[:, c] = (t - row(mu, c)).astype(BF16)
            if last:
                return
            partial_first(1 - role)
        swap(other[:1])
        with jax.named_scope("form_z"):
            partial_z(1 - role)
        swap(other[1:])
        with jax.named_scope("form_own"):
            partial_first(role)
            partial_z(role)

    with jax.named_scope("first"):
        for role in range(2):
            partial_first(role)
            partial_z(role)
    with jax.named_scope("barrier"):
        pl.semaphore_wait(barrier, 2 * peers + 1)

    for role in range(2):
        @pl.when(core == role)
        def _():
            swap(CHUNKS[1 - role])

            def body(s, carry):
                one_step(role, False)
                return carry
            lax.fori_loop(0, NUM_STEPS - 1, body, 0)
            one_step(role, True)


def _write(state, out_h, sem):
    copy = pltpu.make_async_copy(state, out_h, sem)
    copy.start()
    copy.wait()


def solution(mesh):
    feat = mesh.shape["feat"]
    side = math.isqrt(feat // 2)

    def local_run(particles, prec_diag, low_factor, prior_mean, data_mat, labels):
        n, fl = particles.shape
        m = data_mat.shape[0]
        rank = low_factor.shape[1]
        dim = fl * feat
        chips = side * side
        own = n // chips
        peers = chips - 1
        cfg = (side, 256, 2.0 * dim, dim / 4.0, 2.0 / math.sqrt(m * dim))
        dma = pltpu.SemaphoreType.DMA
        every = CHUNKS[0] + CHUNKS[1]
        tall = [own + own // 2 if ch[0] == "g" else own for ch in every]
        wide = [ch[2] if ch[0] == "z" else HALF for ch in every]
        shape = [(chips * h, w) for h, w in zip(tall, wide)]
        slot = [(peers, h, w) for h, w in zip(tall, wide)]
        n_items = len(every)
        state = pl.pallas_call(
            functools.partial(_kernel, cfg),
            out_shape=pltpu.VMEM((n, fl), F32),
            in_specs=[pl.BlockSpec(memory_space=pltpu.HBM)] * 6,
            out_specs=pl.BlockSpec(memory_space=pltpu.VMEM),
            scratch_shapes=[
                pltpu.VMEM((n, fl), F32), pltpu.VMEM((fl,), F32), pltpu.VMEM((fl, rank), BF16),
                pltpu.VMEM((fl,), F32), pltpu.VMEM((m, fl), BF16), pltpu.VMEM((m,), jnp.int32),
                pltpu.VMEM((fl, m), BF16),
                pltpu.VMEM((n, fl), BF16), pltpu.VMEM((n, fl), BF16), pltpu.VMEM((n, n), BF16),
                pltpu.VMEM((n, fl), F32),
                [pltpu.VMEM(s, F32) for s in shape], [pltpu.VMEM(s, F32) for s in shape],
                [pltpu.VMEM(s, F32) for s in slot],
                pltpu.VMEM((n, m), BF16),
                pltpu.VMEM((chips * (own + own // 2), HALF), F32), pltpu.VMEM((n, rank), BF16),
                dma((6,)), dma((len(every),)), dma((len(every),)),
                dma((len(every),)), dma((len(every), peers)),
                dma((n_items,)), dma((n_items, peers)), dma((n_items,)), dma((n_items,)),
            ],
            compiler_params=pltpu.CompilerParams(
                collective_id=0, has_side_effects=True, vmem_limit_bytes=56 * 1024 * 1024),
        )(particles, prec_diag, low_factor, prior_mean, data_mat, labels)
        return pl.pallas_call(
            _write,
            out_shape=jax.ShapeDtypeStruct((n, fl), F32),
            in_specs=[pl.BlockSpec(memory_space=pltpu.VMEM)],
            out_specs=pl.BlockSpec(memory_space=pl.ANY),
            scratch_shapes=[dma],
            compiler_params=pltpu.CompilerParams(vmem_limit_bytes=4 * 1024 * 1024),
        )(state)

    return jax.shard_map(
        local_run,
        mesh=mesh,
        in_specs=(P("ens", "feat"), P(("ens", "feat")), P(("ens", "feat"), None),
                  P(("ens", "feat")), P("ens", "feat"), P("ens")),
        out_specs=P("ens", "feat"),
        check_vma=False,
    )
```

time: 73 us -> 65.1 us (0.89)
  Pallas kernels: 70.3 us -> 64.9 us
  local copies, waits for them, and re-layouts: 2.66 us -> 0 us
    pallas_call x1 -> x2, Pallas kernels: 70.3 us -> 64.9 us  [the longest x1 63.7 us: local_run(): pl.pallas_call(functools.partial(_kernel, cfg), out_shape=pltpu.VMEM((n,...]
    unnamed x1 -> x0, local copies, waits for them, and re-layouts: 2.66 us -> none
where the time goes in v3:
time: 65.1 us
  Pallas kernels  64.9 us (100%)
    pallas_call x1, Pallas kernels, local_run(): pl.pallas_call(functools.partial(_kernel, cfg), out_shape=pltpu.VMEM((n,...  63.7 us

profile of v3, /device:TPU:97, one launch (start us, length us, event | category | flops | bytes accessed | tf_op | source)
XLA Modules:
  0.0 65.1 jit_solution(3966989494947514059)
XLA Ops:
  0.0 63.7 %shard_map.64.state = f32[256,1536]{1,0:T(8,128)S(1)} custom-call(f32[256,1536]{1,0:T(8,128)} %th_h.1, f32[1536]{0:T(1024)} %lam_h.1, bf16[1536,128]{1,0:T(8,128)(2,1)} %u_h.1, f32[1536]{0:T(1024)} %mu_h.1, bf16[768,1536]{1,0:T(8,128)(2,1)} %a_h.1, s32[768]{0:T(1024)} %y_h.1), custom_call_target="tpu_custom_call" | custom-call | tf_op jit(solution)/shard_map/pallas_call | solution.py:315
  63.8 1.2 %shard_map.65 = f32[256,1536]{1,0:T(8,128)} custom-call(f32[256,1536]{1,0:T(8,128)S(1)} %shard_map.64.state), custom_call_target="tpu_custom_call" | custom-call | tf_op jit(solution)/shard_map/pallas_call | solution.py:337

commit v4 on v3

--- a/solution.py
+++ b/solution.py
@@ -32,8 +32,7 @@
     (("q",), ("z", 0, 256), ("z", 512, 128)),
     (("g",), ("z", 256, 256), ("z", 640, 128)),
 )
-DIRECT = tuple(chunks[-1] for chunks in CHUNKS)
-EARLY = 512
+FAR = ((5, 5, 1), (5, 5, 1))
 
 
 def _kernel(cfg, th_h, lam_h, u_h, mu_h, a_h, y_h, out_v,
@@ -60,11 +59,18 @@
 
     to = [chip_at(dx, dy) for dx, dy in hops]
     frm = [chip_at(side - dx, side - dy) for dx, dy in hops]
+    dist = [min(dx, side - dx) + min(dy, side - dy) for dx, dy in hops]
 
     def rows(q, height):
         return pl.ds(pl.multiple_of(q * height, height), height)
 
     ids = {ch: i for i, ch in enumerate(CHUNKS[0] + CHUNKS[1])}
+
+    far = {ch: FAR[role][i] for role in range(2) for i, ch in enumerate(CHUNKS[role])}
+
+    def sends(ch):
+        turn = -1 if ch in CHUNKS[0] else 1
+        return sorted(range(peers), key=lambda k: (-dist[k], turn * hops[k][0], turn * hops[k][1]))
 
     def held(ch):
         if ch[0] == "z":
@@ -99,13 +105,13 @@
     for cp in loads[2:]:
         cp.wait()
     z_at = {}
-    for chunks in CHUNKS:
+    for role, chunks in enumerate(CHUNKS):
         for ch in chunks:
             if ch[0] == "z":
-                z_at[ch] = sum(other[2] for other in z_at)
+                z_at[ch] = sum(c2[2] for c2 in z_at if c2 in chunks)
                 for c in blocks:
                     for j in range(0, ch[2], HALF):
-                        at[c, z_at[ch] + j:z_at[ch] + j + HALF] = a[ch[1] + j:ch[1] + j + HALF, c].T
+                        at[role][c, z_at[ch] + j:z_at[ch] + j + HALF] = a[ch[1] + j:ch[1] + j + HALF, c].T
 
     def partial_first(role):
         p = parts[ids[CHUNKS[role][0]]]
@@ -121,25 +127,26 @@
 
     def partial_z(role):
         zs = CHUNKS[role][1:]
-        start = z_at[zs[0]]
-        width = sum(ch[2] for ch in zs)
-        z = _dot(tb[...], at[:, start:start + width], NN)
+        z = _dot(tb[...], at[role][...], NN)
         for ch in zs:
-            o = z_at[ch] - start
+            o = z_at[ch]
             parts[ids[ch]][...] = z[:, o:o + ch[2]]
 
     def scatter(ch):
         i = ids[ch]
         p, d, r, h = parts[i], others[i], slots[i], height(ch)
         _remote(p, d, dd_s.at[i], dd_r.at[i], partner).wait_recv()
-        for k, q in enumerate(to):
-            p[rows(q, h), :] = p[rows(q, h), :] + d[rows(q, h), :]
-            _remote(p.at[rows(q, h), :], r.at[k], rs_s.at[i], rs_r.at[i, k], q * 2 + core).start()
+        for k in sends(ch):
+            q = to[k]
+            piece = rows(q, h)
+            p[piece, :] = p[piece, :] + d[piece, :]
+            _remote(p.at[piece, :], r.at[k], rs_s.at[i], rs_r.at[i, k], q * 2 + core).start()
 
     def complete(ch):
         i = ids[ch]
         p, d, r, h = parts[i], others[i], slots[i], height(ch)
-        total = p[rows(chip, h), :] + d[rows(chip, h), :]
+        spot = rows(chip, h)
+        total = p[spot, :] + d[spot, :]
         for k in reversed(range(peers)):
             _remote(r.at[k], r.at[k], rs_s.at[i], rs_r.at[i, k], partner).wait_recv()
             total = total + r[k]
@@ -149,42 +156,50 @@
         else:
             done = total.astype(BF16) if ch[0] == "q" else total
         buf = held(ch)
-        buf[rows(chip, h), :] = done
-        mine = buf.at[rows(chip, h), :]
-        for k, q in enumerate(to):
+        buf[spot, :] = done
+        mine = buf.at[spot, :]
+        for k in sends(ch):
+            q = to[k]
             _remote(mine, mine, ag_s.at[i], ag_r.at[i, k], q * 2 + core).start()
-            if ch in DIRECT:
-                _remote(mine, mine, fw_s.at[i], ag_r.at[i, k], q * 2 + 1 - core).start()
+        for k in sends(ch):
+            if dist[k] >= far[ch]:
+                _remote(mine, mine, fw_s.at[i], ag_r.at[i, k], to[k] * 2 + 1 - core).start()
         _remote(mine, mine, fw_s.at[i], fw_r.at[i], partner).start()
 
+    def arrive(ch, k):
+        i, buf = ids[ch], held(ch)
+        piece = buf.at[rows(frm[k], height(ch)), :]
+        _remote(piece, piece, fw_s.at[i], ag_r.at[i, k], partner).wait_recv()
+        return piece
+
     def forward(ch):
-        i, buf, h = ids[ch], held(ch), height(ch)
+        i = ids[ch]
         for k in reversed(range(peers)):
-            piece = buf.at[rows(frm[k], h), :]
-            _remote(piece, piece, fw_s.at[i], ag_r.at[i, k], partner).wait_recv()
-            _remote(piece, piece, fw_s.at[i], fw_r.at[i], partner).start()
-
-    def direct(ch, role):
-        i, buf, h = ids[ch], held(ch), height(ch)
+            piece = arrive(ch, k)
+            if dist[k] < far[ch]:
+                _remote(piece, piece, fw_s.at[i], fw_r.at[i], partner).start()
+
+    def forwarded(ch):
+        i = ids[ch]
+        near = 1 + sum(d < far[ch] for d in dist)
+        part = held(ch).at[pl.ds(0, near * height(ch)), :]
+        _remote(part, part, fw_s.at[i], fw_r.at[i], partner).wait_recv()
         for k in reversed(range(peers)):
-            piece = buf.at[rows(frm[k], h), :]
-            _remote(piece, piece, fw_s.at[i], ag_r.at[i, k], partner).wait_recv()
-        if ch not in CHUNKS[role]:
-            piece = buf.at[rows(chip, h), :]
-            _remote(piece, piece, fw_s.at[i], fw_r.at[i], partner).wait_recv()
-
-    def forwarded(ch):
-        i, buf = ids[ch], held(ch)
-        _remote(buf, buf, fw_s.at[i], fw_r.at[i], partner).wait_recv()
-
-    def drain(ch_own, ch_other):
+            if dist[k] >= far[ch]:
+                arrive(ch, k)
+
+    def drain_sums(ch_own, ch_other):
         for ch in ch_other:
             i = ids[ch]
             _remote(parts[i], parts[i], dd_s.at[i], dd_r.at[i], partner).wait_send()
         for ch in ch_own:
-            i, h, buf = ids[ch], height(ch), held(ch)
+            i, h = ids[ch], height(ch)
             part = parts[i].at[pl.ds(0, peers * h), :]
             _remote(part, part, rs_s.at[i], dd_r.at[i], partner).wait_send()
+
+    def drain_gathers(chs):
+        for ch in chs:
+            i, h, buf = ids[ch], height(ch), held(ch)
             part = buf.at[pl.ds(0, peers * h), :]
             _remote(part, part, ag_s.at[i], fw_r.at[i], partner).wait_send()
             _remote(buf, buf, fw_s.at[i], fw_r.at[i], partner).wait_send()
@@ -217,12 +232,15 @@
 
     def one_step(role, last):
         mine, other = CHUNKS[role], CHUNKS[1 - role]
+        late = min(mine[2][1], other[2][1])
 
         for ch in mine:
             with jax.named_scope(f"scatter_{ch[0]}{ids[ch]}"):
                 scatter(ch)
-        for ch in mine:
-            with jax.named_scope(f"complete_{ch[0]}{ids[ch]}"):
+        with jax.named_scope("complete_first"):
+            complete(mine[0])
+        for ch in mine[1:]:
+            with jax.named_scope(f"complete{ids[ch]}"):
                 complete(ch)
         with jax.named_scope("forward0"):
             forward(mine[0])
@@ -236,19 +254,24 @@
                 th[:, c] = t + (step * 2.0 / (band * n)) * (ksum * t - _dot(kb[...], tb[:, c], NN))
         with jax.named_scope("forward1"):
             forward(mine[1])
+        with jax.named_scope("early_own"):
+            part = slice(mine[1][1], mine[1][1] + mine[1][2])
+            for c in blocks:
+                ps[:, c] = beta * _dot(rz[:, part], a[part, c], NN) - ps[:, c]
         with jax.named_scope("forwarded1"):
             forwarded(other[1])
         with jax.named_scope("early"):
+            part2 = slice(other[1][1], other[1][1] + other[1][2])
             for c in blocks:
-                ps[:, c] = beta * _dot(rz[:, :EARLY], a[:EARLY, c], NN) - ps[:, c]
+                ps[:, c] = ps[:, c] + beta * _dot(rz[:, part2], a[part2, c], NN)
         with jax.named_scope("direct"):
-            direct(mine[2], role)
-            direct(other[2], role)
+            forward(mine[2])
+            forwarded(other[2])
         with jax.named_scope("drain"):
-            drain(mine, other)
+            drain_sums(mine, other)
         with jax.named_scope("update"):
             for c in blocks:
-                score = ps[:, c] + beta * _dot(rz[:, EARLY:], a[EARLY:, c], NN)
+                score = ps[:, c] + beta * _dot(rz[:, late:], a[late:, c], NN)
                 t = th[:, c] + (step / n) * _dot(kb[...], score.astype(BF16), NN)
                 if last:
                     out_v[:, c] = t
@@ -257,6 +280,7 @@
                 tb[:, c] = t.astype(BF16)
                 xb[:, c] = (t - row(mu, c)).astype(BF16)
             if last:
+                drain_gathers(mine)
                 return
             partial_first(1 - role)
         swap(other[:1])
@@ -266,6 +290,7 @@
         with jax.named_scope("form_own"):
             partial_first(role)
             partial_z(role)
+        drain_gathers(mine)
 
     with jax.named_scope("first"):
         for role in range(2):
@@ -320,7 +345,7 @@
             scratch_shapes=[
                 pltpu.VMEM((n, fl), F32), pltpu.VMEM((fl,), F32), pltpu.VMEM((fl, rank), BF16),
                 pltpu.VMEM((fl,), F32), pltpu.VMEM((m, fl), BF16), pltpu.VMEM((m,), jnp.int32),
-                pltpu.VMEM((fl, m), BF16),
+                [pltpu.VMEM((fl, m // 2), BF16)] * 2,
                 pltpu.VMEM((n, fl), BF16), pltpu.VMEM((n, fl), BF16), pltpu.VMEM((n, n), BF16),
                 pltpu.VMEM((n, fl), F32),
                 [pltpu.VMEM(s, F32) for s in shape], [pltpu.VMEM(s, F32) for s in shape],

time: 65.1 us -> 64.4 us (0.989)
  Pallas kernels: 64.9 us -> 64.2 us
    pallas_call x1, Pallas kernels: 63.7 us -> 63 us  [local_run(): pl.pallas_call(functools.partial(_kernel, cfg), out_shape=pltpu.VMEM((n,...]
where the time goes in v4:
time: 64.4 us
  Pallas kernels  64.2 us (100%)
    pallas_call x1, Pallas kernels, local_run(): pl.pallas_call(functools.partial(_kernel, cfg), out_shape=pltpu.VMEM((n,...  63 us

profile of v4, /device:TPU:97, one launch (start us, length us, event | category | flops | bytes accessed | tf_op | source)
XLA Modules:
  0.0 64.4 jit_solution(14331227117177558758)
XLA Ops:
  0.0 63.0 %shard_map.64.state = f32[256,1536]{1,0:T(8,128)S(1)} custom-call(f32[256,1536]{1,0:T(8,128)} %th_h.1, f32[1536]{0:T(1024)} %lam_h.1, bf16[1536,128]{1,0:T(8,128)(2,1)} %u_h.1, f32[1536]{0:T(1024)} %mu_h.1, bf16[768,1536]{1,0:T(8,128)(2,1)} %a_h.1, s32[768]{0:T(1024)} %y_h.1), custom_call_target="tpu_custom_call" | custom-call | tf_op jit(solution)/shard_map/pallas_call | solution.py:340
  63.0 1.2 %shard_map.65 = f32[256,1536]{1,0:T(8,128)} custom-call(f32[256,1536]{1,0:T(8,128)S(1)} %shard_map.64.state), custom_call_target="tpu_custom_call" | custom-call | tf_op jit(solution)/shard_map/pallas_call | solution.py:362

commit v5 on v4

--- a/solution.py
+++ b/solution.py
@@ -32,7 +32,7 @@
     (("q",), ("z", 0, 256), ("z", 512, 128)),
     (("g",), ("z", 256, 256), ("z", 640, 128)),
 )
-FAR = ((5, 5, 1), (5, 5, 1))
+FAR = ((5, 4, 1), (5, 4, 1))
 
 
 def _kernel(cfg, th_h, lam_h, u_h, mu_h, a_h, y_h, out_v,

time: 64.4 us -> 64.3 us (level)
  no operation moved by 1% of the time
where the time goes in v5:
time: 64.3 us; the launch traced here: 64.2 us
  Pallas kernels  64 us (100%)
    pallas_call x1, Pallas kernels, local_run(): pl.pallas_call(functools.partial(_kernel, cfg), out_shape=pltpu.VMEM((n,...  62.9 us

profile of v5, /device:TPU:97, one launch (start us, length us, event | category | flops | bytes accessed | tf_op | source)
XLA Modules:
  0.0 64.2 jit_solution(11277010981285595436)
XLA Ops:
  0.0 62.9 %shard_map.64.state = f32[256,1536]{1,0:T(8,128)S(1)} custom-call(f32[256,1536]{1,0:T(8,128)} %th_h.1, f32[1536]{0:T(1024)} %lam_h.1, bf16[1536,128]{1,0:T(8,128)(2,1)} %u_h.1, f32[1536]{0:T(1024)} %mu_h.1, bf16[768,1536]{1,0:T(8,128)(2,1)} %a_h.1, s32[768]{0:T(1024)} %y_h.1), custom_call_target="tpu_custom_call" | custom-call | tf_op jit(solution)/shard_map/pallas_call | solution.py:340
  62.9 1.2 %shard_map.65 = f32[256,1536]{1,0:T(8,128)} custom-call(f32[256,1536]{1,0:T(8,128)S(1)} %shard_map.64.state), custom_call_target="tpu_custom_call" | custom-call | tf_op jit(solution)/shard_map/pallas_call | solution.py:362
